TPU v7x, 256 devices: a whole 4x4x8 slice. The times are simulated.
256 devices in a mesh: batch: 128 (over z, y, x_lo, core), rep: 2 (over x_hi).
Axes of the slice: x: 4 (x_hi: 2, x_lo: 2; x = x_hi * 2 + x_lo), y: 4, z: 8, core: 2. Of those that a mesh axis runs over, the one named last changes fastest.
Arguments:
- queries: bfloat16 [16384, 512], P('batch', 'rep'), may hold values from -8 to 8
- passages: bfloat16 [16384, 512], P('batch', 'rep'), may hold values from -8 to 8
- positives: int32 [16384], replicated, may hold values from 0 to 16383, each once
Outputs:
- grad_queries: float32 [16384, 512], P('batch', 'rep')
- grad_passages: float32 [16384, 512], P('batch', 'rep')
Inputs may be any that keep to these rules, and one draw needn't show every extreme that they name: `positives`: each passage is the positive of exactly one query.
All inputs are finite; a program needn't handle non-finite values.
Results may differ from a plain program's by a relative error of at most 0.0013.
Values may be sent and summed in bfloat16 or wider, within the bound.
A program may use at most 128 MiB of HBM per device.

v0:
```python
import math
import jax
import jax.numpy as jnp
from jax import lax
from jax.sharding import Mesh
from jax.sharding import PartitionSpec as P

BATCH = ("batch_0", "batch_1", "batch_2", "batch_3")
NEGATIVE = -1e30


def sent_together(arrays, axis, dim, along):
    both = jnp.concatenate(arrays, axis=along)
    filled, at, outs = (lax.all_gather(both, axis, axis=dim, tiled=True), 0, [])
    for a in arrays:
        outs.append(lax.slice_in_dim(filled, at, at + a.shape[along], axis=along))
        at += a.shape[along]
    return tuple(outs)


def copy_for_each(x, axis):
    count = lax.axis_size(axis)
    return lax.all_to_all(jnp.broadcast_to(x[None], (count, *x.shape)), axis, 0, 0, tiled=True)


def gathered_once(x, axis):
    leaves = jax.tree.leaves(x)
    order = sorted(range(len(leaves)), key=lambda k: -leaves[k].size)
    width = (1, *leaves[order[0]].shape)[-1]
    lines = [
        jnp.pad(leaves[k].reshape(-1), (0, -leaves[k].size % width)).reshape(-1, width)
        for k in order
    ]
    both, at, found = (copy_for_each(jnp.concatenate(lines), axis), 0, {})
    for k, line in zip(order, lines):
        section = both[:, at : at + len(line)].reshape(len(both), -1)
        found[k] = section[:, : leaves[k].size].reshape(-1, *leaves[k].shape)
        at += len(line)
    numbers = iter(range(len(leaves)))
    return jax.tree.map(lambda _: found[next(numbers)], x)


def combined_pairwise(pieces, combine):
    while len(jax.tree.leaves(pieces)[0]) > 1:
        pieces = jax.vmap(combine)(
            *(jax.tree.map(lambda part: part[side::2], pieces) for side in (0, 1))
        )
    return jax.tree.map(lambda part: part[0], pieces)


def joined_all(x, axis, combine):
    pieces = gathered_once(x, axis)
    return combined_pairwise(pieces, combine)


def collected_together(x, axis):
    leaves = jax.tree.leaves(x)
    order = sorted(range(len(leaves)), key=lambda k: -leaves[k].size)
    width = (1, *leaves[order[0]].shape)[-1]
    lines = [
        jnp.pad(leaves[k].reshape(-1), (0, -leaves[k].size % width)).reshape(-1, width)
        for k in order
    ]
    both, at, found = (lax.all_gather(jnp.concatenate(lines), axis), 0, {})
    for k, line in zip(order, lines):
        section = both[:, at : at + len(line)].reshape(len(both), -1)
        found[k] = section[:, : leaves[k].size].reshape(-1, *leaves[k].shape)
        at += len(line)
    numbers = iter(range(len(leaves)))
    return jax.tree.map(lambda _: found[next(numbers)], x)


def merged_by_axis(x, axes, combine):
    for axis in axes:
        pieces = collected_together(x, axis)
        x = jax.tree.map(lambda part: part[0], pieces)
        for k in range(1, lax.axis_size(axis)):
            x = combine(x, jax.tree.map(lambda part: part[k], pieces))
    return x


def joined_along(pieces, dim):
    pieces = jnp.moveaxis(pieces, 0, dim)
    dims = pieces.shape
    return pieces.reshape(*dims[:dim], dims[dim] * dims[dim + 1], *dims[dim + 2 :])


def stacked_from(x, axes, order):
    pieces = x
    for k in order:
        pieces = lax.all_gather(pieces, axes[k])
    done = order[::-1]
    back = [done.index(k) for k in range(len(axes))]
    pieces = pieces.transpose(*back, *range(len(axes), pieces.ndim))
    return pieces.reshape(-1, *x.shape)


def whole_of(x, axes, order, dim):
    return joined_along(stacked_from(x, axes, order), dim)


def collect(x, axis, dim):
    pieces = copy_for_each(x, axis)
    return joined_along(pieces, dim)


def in_blocks(x, dim, count):
    dims = x.shape
    pieces = x.reshape(*dims[:dim], count, dims[dim] // count, *dims[dim + 1 :])
    return jnp.moveaxis(pieces, dim, 0)


def summed_on_arrival(x, axis, dim):
    count = lax.axis_size(axis)
    pieces = lax.all_to_all(in_blocks(x, dim, count), axis, 0, 0, tiled=True)
    return jnp.sum(pieces, axis=0)


def sent_together_2(arrays, axis, dim, along):
    both = jnp.concatenate(arrays, axis=along)
    filled, at, outs = (summed_on_arrival(both, axis, dim), 0, [])
    for a in arrays:
        outs.append(lax.slice_in_dim(filled, at, at + a.shape[along], axis=along))
        at += a.shape[along]
    return tuple(outs)


def sweep_blocks(update, running, members):
    piece_rows = members[0].shape[0]

    def advance(carried, block_index):
        sliced = tuple(
            (lax.dynamic_slice_in_dim(member, block_index * 512, 512, 0) for member in members)
        )
        return (update(carried, sliced, block_index * 512), None)

    running, unused = lax.scan(advance, running, jnp.arange(piece_rows // 512, dtype=jnp.int32))
    return running


def combine_pairs(former, latter):
    results = []
    for position in range(0, len(former), 2):
        highest = jnp.maximum(former[position], latter[position])
        summed = former[position + 1] * jnp.exp(former[position] - highest) + latter[
            position + 1
        ] * jnp.exp(latter[position] - highest)
        results.extend([highest, summed])
    return tuple(results)


def pair_scores(local_set, remote_set, logit_scale):
    products = lax.dot_general(
        local_set, remote_set, (((1,), (1,)), ((), ())), preferred_element_type=jnp.float32
    )
    return products * logit_scale


def weighted_sum(
    local_set, local_norm, local_keys, remote_set, remote_norm, remote_keys, logit_scale
):
    scores = pair_scores(local_set, remote_set, logit_scale)
    matches = (local_keys[:, None] == remote_keys[None, :]).astype(jnp.float32)
    weights = (
        jnp.exp(scores - local_norm[:, None])
        + jnp.exp(scores - remote_norm[None, :])
        - 2.0 * matches
    )
    return jnp.dot(weights.astype(jnp.bfloat16), remote_set, preferred_element_type=jnp.float32)


def local(queries, passages, positives):
    own_rows = queries.shape[0]
    half_rows = own_rows // 2
    model_width = queries.shape[1] * lax.axis_size("rep")
    batch_count = lax.axis_size(BATCH)
    all_rows = batch_count * own_rows
    column_count = batch_count * half_rows
    logit_scale = 1.0 / math.sqrt(model_width)
    batch_index = lax.axis_index(BATCH)
    rep_index = lax.axis_index("rep")
    block_start = batch_index * own_rows
    half_start = rep_index * half_rows
    query_full, passage_full = sent_together((queries, passages), "rep", 1, 0)
    passage_half = lax.dynamic_slice_in_dim(passage_full, half_start, half_rows, 0)

    def score_update(running, sliced, offset):
        row_high, row_total, column_high, column_total = running
        scores = pair_scores(query_full, sliced[0], logit_scale)
        new_high = jnp.maximum(row_high, jnp.max(scores, axis=1))
        row_total = row_total * jnp.exp(row_high - new_high) + jnp.sum(
            jnp.exp(scores - new_high[:, None]), axis=1
        )
        piece_high = jnp.max(scores, axis=0)
        piece_total = jnp.sum(jnp.exp(scores - piece_high[None, :]), axis=0)
        column_high = lax.dynamic_update_slice_in_dim(column_high, piece_high, offset, 0)
        column_total = lax.dynamic_update_slice_in_dim(column_total, piece_total, offset, 0)
        return (new_high, row_total, column_high, column_total)

    starting = (
        jnp.full((own_rows,), NEGATIVE, jnp.float32),
        jnp.zeros((own_rows,), jnp.float32),
        jnp.full((column_count,), NEGATIVE, jnp.float32),
        jnp.zeros((column_count,), jnp.float32),
    )
    row_high, row_total, column_high, column_total = sweep_blocks(
        score_update, starting, (lax.all_gather(passage_half, BATCH, axis=0, tiled=True),)
    )
    row_high, row_total = joined_all((row_high, row_total), "rep", combine_pairs)
    column_high, column_total = merged_by_axis((column_high, column_total), BATCH, combine_pairs)
    row_norms = whole_of(row_high + jnp.log(row_total), BATCH, (2, 0, 1, 3), 0)
    column_halves = collect(column_high + jnp.log(column_total), "rep", 0)
    column_norms = (
        column_halves.reshape(2, batch_count, half_rows).transpose(1, 0, 2).reshape(all_rows)
    )
    row_own = lax.dynamic_slice_in_dim(row_norms, block_start, own_rows, 0)
    column_own = lax.dynamic_slice_in_dim(column_norms, block_start, own_rows, 0)
    positive_own = lax.dynamic_slice_in_dim(positives, block_start, own_rows, 0)
    own_ids = block_start + jnp.arange(own_rows, dtype=jnp.int32)
    all_ids = jnp.arange(all_rows, dtype=jnp.int32)
    cleared = jnp.zeros((own_rows, model_width), jnp.float32)

    def half_order(vector):
        return lax.dynamic_slice_in_dim(
            vector.reshape(batch_count, own_rows), half_start, half_rows, 1
        ).reshape(column_count)

    column_order = half_order(column_norms)
    row_order = half_order(row_norms)
    positive_order = half_order(positives)
    passage_order = half_order(all_ids)
    query_half = lax.dynamic_slice_in_dim(query_full, half_start, half_rows, 0)

    def both_update(running, sliced, offset):
        query_sum, passage_sum = running
        passage_piece, query_piece = sliced
        piece_rows = passage_piece.shape[0]

        def window(vector):
            return lax.dynamic_slice_in_dim(vector, offset, piece_rows, 0)

        query_sum = query_sum + weighted_sum(
            query_full,
            row_own,
            positive_own,
            passage_piece,
            window(column_order),
            window(passage_order),
            logit_scale,
        )
        passage_sum = passage_sum + weighted_sum(
            passage_full,
            column_own,
            own_ids,
            query_piece,
            window(row_order),
            window(positive_order),
            logit_scale,
        )
        return (query_sum, passage_sum)

    query_sum, passage_sum = sweep_blocks(
        both_update, (cleared, cleared), sent_together((passage_half, query_half), BATCH, 0, 1)
    )
    grad_queries, grad_passages = sent_together_2(
        (query_sum * logit_scale, passage_sum * logit_scale), "rep", 1, 0
    )
    return (grad_queries, grad_passages)


def solution(mesh):
    split = Mesh(
        mesh.devices.reshape(8, 4, 2, 2, mesh.shape["rep"]),
        ("batch_0", "batch_1", "batch_2", "batch_3", "rep"),
    )
    return jax.shard_map(
        local,
        mesh=split,
        in_specs=(P(BATCH, "rep"), P(BATCH, "rep"), P()),
        out_specs=(P(BATCH, "rep"), P(BATCH, "rep")),
        check_vma=False,
    )
```

profile of v0, /device:TPU:32, one launch (start us, length us, event | category | flops | bytes accessed | tf_op | source)
XLA Modules:
  0.0 585.7 jit_solution(4580716487339270084)
XLA Ops:
  8.1 7.4 %all_gather.55 = bf16[256,512]{1,0:T(8,128)(2,1)S(1)} all-gather(bf16[256,256]{1,0:T(8,128)(2,1)S(1)} %pad_maximum_fusion.1), channel_id=1, replica_groups=mesh['batch_0'=8,'batch_1'=4,'batch_2'=2,'batch_3'=2,'rep'=2] {'rep'}, dimensions={1}, use_global_device_ids=true | all-gather | bytes 393216 | tf_op jit(solution)/shard_map/all_gather | solution.py:14
  19.7 219.5 %all-gather.18.cloned.1.call-done = bf16[8192,512]{1,0:T(8,128)(2,1)} async-done(((bf16[64,512]{1,0:T(8,128)(2,1)}), bf16[8192,512]{1,0:T(8,128)(2,1)}) %all-gather.18.cloned.1.call-update) | async-done | bytes 8388624 | tf_op jit(solution)/shard_map/all_gather | solution.py:207
  239.2 55.7 %while.30 = (s32[]{:T(128)}, f32[128]{0:T(128)S(1)}, f32[128]{0:T(128)S(1)}, f32[8192]{0:T(1024)S(1)}, f32[8192]{0:T(1024)S(1)}, /*index=5*/s32[16]{0:T(128)S(1)...) while((s32[]{:T(128)}, f32[128]{0:T(128)S(1)}, ...), condition=%wide.region_5.6_spmd.clone, body=%wide.region_0.5_spmd.clone.sunk | while | flops 67567240 | bytes 1200838 | solution.py:137
  295.5 4.3 all-to-all-start
  299.9 25.0 %all-gather.9 = f32[8,2,8192]{2,1,0:T(2,128)S(1)} all-gather(f32[1,2,8192]{2,1,0:T(2,128)S(1)} %maximum_bitcast_fusion), channel_id=5, replica_groups=mesh['batch_0'=8,'batch_1'=4,'batch_2'=2,'batch_3'=2,'rep'=2] {'batch_0'}, dimensions={0}, use_global_device_ids=true | all-gather | bytes 589824 | tf_op jit(solution)/shard_map/all_gather | solution.py:64
  325.8 12.3 %all-gather.10 = f32[4,2,8192]{2,1,0:T(2,128)S(1)} all-gather(f32[1,2,8192]{2,1,0:T(2,128)S(1)} %maximum_bitcast_fusion.1), channel_id=6, replica_groups=mesh['batch_0'=8,'batch_1'=4,'batch_2'=2,'batch_3'=2,'rep'=2] {'batch_1'}, dimensions={0}, use_global_device_ids=true | all-gather | bytes 327680 | tf_op jit(solution)/shard_map/all_gather | solution.py:64
  338.4 4.9 all-gather.11
  343.5 1.9 all-gather.12
  346.3 5.0 all-to-all-start.1
  351.3 4.2 all-gather.7
  355.5 14.3 %all-gather.8 = f32[8,2,128]{2,1,0:T(2,128)S(1)} all-gather(f32[1,2,128]{2,1,0:T(2,128)S(1)} %bitcast.357), channel_id=2, replica_groups=mesh['batch_0'=8,'batch_1'=4,'batch_2'=2,'batch_3'=2,'rep'=2] {'batch_0'}, dimensions={0}, use_global_device_ids=true | all-gather | bytes 9216 | tf_op jit(solution)/shard_map/all_gather | solution.py:91
  369.8 11.9 %all-gather.1 = f32[32,2,128]{2,1,0:T(2,128)S(1)} all-gather(f32[8,2,128]{2,1,0:T(2,128)S(1)} %all-gather.8), channel_id=3, replica_groups=mesh['batch_0'=8,'batch_1'=4,'batch_2'=2,'batch_3'=2,'rep'=2] {'batch_1'}, dimensions={0}, use_global_device_ids=true | all-gather | bytes 40960 | tf_op jit(solution)/shard_map/all_gather | solution.py:91
  384.8 83.6 %all-gather.16.cloned.1.call-done = bf16[8192,1024]{1,0:T(8,128)(2,1)} async-done(((bf16[64,1024]{1,0:T(8,128)(2,1)}), bf16[8192,1024]{1,0:T(8,128)(2,1)}) %all-gather.16.cloned.1.call-update) | async-done | bytes 16777232 | tf_op jit(solution)/shard_map/all_gather | solution.py:14
  468.4 11.3 %fusion.101 = (bf16[8192,512]{1,0:T(8,128)(2,1)}, bf16[8192,512]{1,0:T(8,128)(2,1)}) fusion(bf16[8192,1024]{1,0:T(8,128)(2,1)} %all-gather.16.cloned.1.call-done), kind=kLoop, calls=%fused_computation.152 | loop fusion | bytes 33554432 | tf_op jit(solution)/shard_map/slice | solution.py:16
  479.7 86.1 %while.31 = (s32[]{:T(128)}, f32[128,512]{1,0:T(8,128)S(1)}, f32[128,512]{1,0:T(8,128)S(1)}, s32[16]{0:T(128)S(1)}, bf16[8192,512]{1,0:T(8,128)(2,1)}, /*index=5...) while((s32[]{:T(128)}, f32[128,512]{1,0:T(8,128)S(1)}, ...), condition=%wide.region_7.8_spmd.clone, body=%wide.region_6.7_spmd.clone.sunk | while | flops 269746304 | bytes 3438348 | solution.py:137
  481.1 2.0 convolution_add_fusion.5
  483.3 1.9 convolution_add_fusion.4
  486.6 1.9 convolution_add_fusion.5
  488.6 1.9 convolution_add_fusion.4
  492.0 1.9 convolution_add_fusion.5
  494.0 1.9 convolution_add_fusion.4
  497.3 1.9 convolution_add_fusion.5
  499.4 1.9 convolution_add_fusion.4
  502.7 1.9 convolution_add_fusion.5
  504.7 1.9 convolution_add_fusion.4
  508.1 1.9 convolution_add_fusion.5
  510.2 1.9 convolution_add_fusion.4
  513.5 1.9 convolution_add_fusion.5
  515.5 1.9 convolution_add_fusion.4
  518.8 1.9 convolution_add_fusion.5
  520.9 1.9 convolution_add_fusion.4
  524.2 1.9 convolution_add_fusion.5
  526.2 1.9 convolution_add_fusion.4
  529.5 1.9 convolution_add_fusion.5
  531.6 1.9 convolution_add_fusion.4
  534.9 1.9 convolution_add_fusion.5
  537.0 1.9 convolution_add_fusion.4
  540.3 1.9 convolution_add_fusion.5
  542.4 1.9 convolution_add_fusion.4
  545.7 1.9 convolution_add_fusion.5
  547.7 1.9 convolution_add_fusion.4
  551.1 1.9 convolution_add_fusion.5
  553.1 1.9 convolution_add_fusion.4
  556.4 1.9 convolution_add_fusion.5
  558.5 1.9 convolution_add_fusion.4
  561.8 1.9 convolution_add_fusion.5
  563.8 1.9 convolution_add_fusion.4
  566.4 11.7 %all_to_all.16 = f32[2,256,256]{2,1,0:T(8,128)S(1)} all-to-all(f32[2,256,256]{2,1,0:T(8,128)S(1)} %copy.28), channel_id=1, replica_groups=mesh['batch_0'=8,'batch_1'=4,'batch_2'=2,'batch_3'=2,'rep'=2] {'rep'}, dimensions={0} | all-to-all | bytes 1048576 | tf_op jit(solution)/shard_map/all_to_all | solution.py:115
  (283 shorter events, 71.2 us)
Async XLA Ops:
  7.2 232.0 %all-gather.18.cloned.1.call-start = ((), (), s32[]{:S(2)}) async-start(), calls=%async_computation.4 | async-start | bytes 8454144 | tf_op jit(solution)/shard_map/all_gather | solution.py:207
  16.2 452.2 %all-gather.16.cloned.1.call-start = ((), (), s32[]{:S(2)}) async-start(), calls=%async_computation.3 | async-start | bytes 16908288 | tf_op jit(solution)/shard_map/all_gather | solution.py:14
  295.5 50.1 %all-to-all-start = ((f32[2,2,128]{2,1,0:T(2,128)}), f32[2,2,128]{2,1,0:T(2,128)S(1)}, u32[]{:S(2)}, u32[]{:S(2)}) async-start(f32[2,2,128]{2,1,0:T(2,128)} %broadcast_in_dim.21), calls=%async_computation | async-start | bytes 4096 | tf_op jit(solution)/shard_map/all_to_all | solution.py:23
  346.3 37.6 %all-to-all-start.1 = ((f32[2,1,8192]{2,1,0:T(1,128)}), f32[2,1,8192]{2,1,0:T(1,128)S(1)}, u32[]{:S(2)}, u32[]{:S(2)}) async-start(f32[2,1,8192]{2,1,0:T(1,128)} %broadcast_in_dim.22), calls=%async_computation.1 | async-start | bytes 131072 | tf_op jit(solution)/shard_map/all_to_all | solution.py:23
Sparse Core Ops, SparseCore 0:
  16.3 222.8 all-gather.17
  241.6 226.7 all-gather.15
where the time goes:
time: 588 us; the launch traced here: 586 us
  waiting for transfers between devices  303 us (52%)
  blocking collectives  95.6 us (16%)
  matrix products  83.6 us (14%)
  local copies, waits for them, and re-layouts  48.4 us (8%)
  loops' own time  22 us (4%)
  between operations  14.3 us (2%)
  starting transfers between devices  9.39 us (2%)
  other arithmetic  9.37 us (2%)
    all_gather x1, waiting for transfers between devices, local(): lax.all_gather(passage_half, BATCH, axis=0, tiled=True)  220 us
    all_gather x1, waiting for transfers between devices, sent_together(): filled, at, outs = (lax.all_gather(both, axis, axis=dim, tiled=True), 0, [])  83.6 us
    dot_general x32, matrix products, weighted_sum(): jnp.dot(weights.astype(jnp.bfloat16), remote_set, preferred_element_type=...  60.7 us
    all_gather x4, blocking collectives, collected_together(): both, at, found = (lax.all_gather(jnp.concatenate(lines), axis), 0, {})  44.1 us
    all_gather x4, blocking collectives, stacked_from(): pieces = lax.all_gather(pieces, axes[k])  32.3 us
    dot_general x16, matrix products, pair_scores(): lax.dot_general(local_set, remote_set, (((1,), (1,)), ((), ())), preferre...  22.8 us
    another operation x2, loops' own time, sweep_blocks(): lax.scan(advance, running, jnp.arange(piece_rows // 512, dtype=jnp.int32))  22 us
    dynamic_slice x32, local copies, waits for them, and re-layouts, sweep_blocks(): lax.scan(advance, running, jnp.arange(piece_rows // 512, dtype=jnp.int32))  18.8 us
  transfers between devices with their start and end apart: 4, of which 2 were waited for; matrix products, arithmetic and copies ran while one was open for 9% of the time, Pallas kernels for 0%

commit v1 on v0

--- a/solution.py
+++ b/solution.py
@@ -1,3 +1,4 @@
+import functools
 import math
 import jax
 import jax.numpy as jnp
@@ -7,6 +8,21 @@
 
 BATCH = ("batch_0", "batch_1", "batch_2", "batch_3")
 NEGATIVE = -1e30
+
+
+def drive_tiles(array_in, named_axis, ndim_at):
+    return jnp.concatenate(
+        lax.all_to_all(
+            jnp.stack([array_in] * lax.psum(1, axis_name=named_axis)),
+            axis_name=named_axis,
+            split_axis=0,
+            concat_axis=0,
+        ),
+        axis=ndim_at,
+    )
+
+
+_link_lots_all = functools.partial(drive_tiles, named_axis=BATCH, ndim_at=0)
 
 
 def sent_together(arrays, axis, dim, along):
@@ -204,7 +220,7 @@
         jnp.zeros((column_count,), jnp.float32),
     )
     row_high, row_total, column_high, column_total = sweep_blocks(
-        score_update, starting, (lax.all_gather(passage_half, BATCH, axis=0, tiled=True),)
+        score_update, starting, (_link_lots_all(passage_half),)
     )
     row_high, row_total = joined_all((row_high, row_total), "rep", combine_pairs)
     column_high, column_total = merged_by_axis((column_high, column_total), BATCH, combine_pairs)

time: 588 us -> 535 us (0.910)
  waiting for transfers between devices: 303 us -> 234 us
  starting transfers between devices: 9.39 us -> 22.8 us
    all_to_all x0 -> x1, waiting for transfers between devices: none -> 234 us  [drive_tiles(): lax.all_to_all(jnp.stack([array_in] * lax.psum(1, axis_name=named_axis)),...]
    all_gather x1 -> x0, waiting for transfers between devices: 220 us -> none  [local(): lax.all_gather(passage_half, BATCH, axis=0, tiled=True)]
    all_gather x1, waiting for transfers between devices: 83.6 us -> 0.01 us  [sent_together(): filled, at, outs = (lax.all_gather(both, axis, axis=dim, tiled=True), 0, [])]
    all_to_all x0 -> x1, starting transfers between devices: none -> 14.1 us  [drive_tiles(): lax.all_to_all(jnp.stack([array_in] * lax.psum(1, axis_name=named_axis)),...]
  transfers between devices with their start and end apart: 4 -> 4, of which waited for: 2 -> 1; matrix products, arithmetic and copies ran while one was open for 9% -> 9% of each run, Pallas kernels for 0% -> 0%
where the time goes in v1:
time: 535 us; the launch traced here: 531 us
  waiting for transfers between devices  234 us (44%)
  blocking collectives  97.7 us (18%)
  matrix products  83.5 us (16%)
  local copies, waits for them, and re-layouts  50.9 us (10%)
  starting transfers between devices  22.8 us (4%)
  loops' own time  20.4 us (4%)
  between operations  14.3 us (3%)
  other arithmetic  7.69 us (1%)
    all_to_all x1, waiting for transfers between devices, drive_tiles(): lax.all_to_all(jnp.stack([array_in] * lax.psum(1, axis_name=named_axis)),...  234 us
    dot_general x32, matrix products, weighted_sum(): jnp.dot(weights.astype(jnp.bfloat16), remote_set, preferred_element_type=...  60.7 us
    all_gather x4, blocking collectives, collected_together(): both, at, found = (lax.all_gather(jnp.concatenate(lines), axis), 0, {})  43.3 us
    all_gather x4, blocking collectives, stacked_from(): pieces = lax.all_gather(pieces, axes[k])  32.6 us
    dot_general x16, matrix products, pair_scores(): lax.dot_general(local_set, remote_set, (((1,), (1,)), ((), ())), preferre...  22.8 us
    another operation x2, loops' own time, sweep_blocks(): lax.scan(advance, running, jnp.arange(piece_rows // 512, dtype=jnp.int32))  20.4 us
    dynamic_slice x32, local copies, waits for them, and re-layouts, sweep_blocks(): lax.scan(advance, running, jnp.arange(piece_rows // 512, dtype=jnp.int32))  18.3 us
    all_to_all x1, blocking collectives, summed_on_arrival(): pieces = lax.all_to_all(in_blocks(x, dim, count), axis, 0, 0, tiled=True)  14.4 us
  transfers between devices with their start and end apart: 4, of which 1 were waited for; matrix products, arithmetic and copies ran while one was open for 9% of the time, Pallas kernels for 0%

profile of v1, /device:TPU:32, one launch (start us, length us, event | category | flops | bytes accessed | tf_op | source)
XLA Modules:
  0.0 531.2 jit_solution(10713568677704161086)
XLA Ops:
  8.1 7.4 %all_gather.52 = bf16[256,512]{1,0:T(8,128)(2,1)S(1)} all-gather(bf16[256,256]{1,0:T(8,128)(2,1)S(1)} %pad_maximum_fusion.1), channel_id=1, replica_groups=mesh['batch_0'=8,'batch_1'=4,'batch_2'=2,'batch_3'=2,'rep'=2] {'rep'}, dimensions={1}, use_global_device_ids=true | all-gather | bytes 393216 | tf_op jit(solution)/shard_map/all_gather | solution.py:30
  15.5 4.3 stack.2
  19.8 14.1 %all-to-all-start = ((bf16[128,64,512]{2,1,0:T(8,128)(2,1)}), bf16[128,64,512]{2,1,0:T(8,128)(2,1)}, u32[]{:S(2)}, u32[]{:S(2)}) async-start(bf16[128,64,512]{2,1,0:T(8,128)(2,1)} %stack.2), calls=%async_computation | async-start | bytes 16777216 | tf_op jit(solution)/shard_map/all_to_all | solution.py:15
  35.0 234.1 %all-to-all-done = bf16[128,64,512]{2,1,0:T(8,128)(2,1)} async-done(((bf16[128,64,512]{2,1,0:T(8,128)(2,1)}), bf16[128,64,512]{2,1,0:T(8,128)(2,1)}, u32[]{:S(2)}, u32[]{:S(2)}) %all-to-all-start) | async-done | bytes 8388640 | tf_op jit(solution)/shard_map/all_to_all | solution.py:15
  269.0 53.6 %while.30 = (s32[]{:T(128)}, f32[128]{0:T(128)S(1)}, f32[128]{0:T(128)S(1)}, f32[8192]{0:T(1024)S(1)}, f32[8192]{0:T(1024)S(1)}, /*index=5*/s32[16]{0:T(128)S(1)...) while((s32[]{:T(128)}, f32[128]{0:T(128)S(1)}, ...), condition=%wide.region_5.6_spmd.clone, body=%wide.region_0.5_spmd.clone.sunk | while | flops 67567240 | bytes 1200838 | solution.py:153
  323.2 3.9 all-to-all-start.1
  327.2 24.2 %all-gather.9 = f32[8,2,8192]{2,1,0:T(2,128)S(1)} all-gather(f32[1,2,8192]{2,1,0:T(2,128)S(1)} %maximum_bitcast_fusion), channel_id=5, replica_groups=mesh['batch_0'=8,'batch_1'=4,'batch_2'=2,'batch_3'=2,'rep'=2] {'batch_0'}, dimensions={0}, use_global_device_ids=true | all-gather | bytes 589824 | tf_op jit(solution)/shard_map/all_gather | solution.py:80
  352.2 12.3 %all-gather.10 = f32[4,2,8192]{2,1,0:T(2,128)S(1)} all-gather(f32[1,2,8192]{2,1,0:T(2,128)S(1)} %maximum_bitcast_fusion.1), channel_id=6, replica_groups=mesh['batch_0'=8,'batch_1'=4,'batch_2'=2,'batch_3'=2,'rep'=2] {'batch_1'}, dimensions={0}, use_global_device_ids=true | all-gather | bytes 327680 | tf_op jit(solution)/shard_map/all_gather | solution.py:80
  364.9 4.9 all-gather.11
  370.0 1.9 all-gather.12
  372.8 4.7 all-to-all-start.2
  377.5 4.2 all-gather.7
  381.7 14.6 %all-gather.8 = f32[8,2,128]{2,1,0:T(2,128)S(1)} all-gather(f32[1,2,128]{2,1,0:T(2,128)S(1)} %bitcast.358), channel_id=2, replica_groups=mesh['batch_0'=8,'batch_1'=4,'batch_2'=2,'batch_3'=2,'rep'=2] {'batch_0'}, dimensions={0}, use_global_device_ids=true | all-gather | bytes 9216 | tf_op jit(solution)/shard_map/all_gather | solution.py:107
  396.3 11.9 %all-gather.1 = f32[32,2,128]{2,1,0:T(2,128)S(1)} all-gather(f32[8,2,128]{2,1,0:T(2,128)S(1)} %all-gather.8), channel_id=3, replica_groups=mesh['batch_0'=8,'batch_1'=4,'batch_2'=2,'batch_3'=2,'rep'=2] {'batch_1'}, dimensions={0}, use_global_device_ids=true | all-gather | bytes 40960 | tf_op jit(solution)/shard_map/all_gather | solution.py:107
  411.3 11.3 %fusion.101 = (bf16[8192,512]{1,0:T(8,128)(2,1)}, bf16[8192,512]{1,0:T(8,128)(2,1)}) fusion(bf16[8192,1024]{1,0:T(8,128)(2,1)} %all-gather.15.cloned.1.call-done), kind=kLoop, calls=%fused_computation.152 | loop fusion | bytes 33554432 | tf_op jit(solution)/shard_map/slice | solution.py:32
  422.6 86.1 %while.31 = (s32[]{:T(128)}, f32[128,512]{1,0:T(8,128)S(1)}, f32[128,512]{1,0:T(8,128)S(1)}, s32[16]{0:T(128)S(1)}, bf16[8192,512]{1,0:T(8,128)(2,1)}, /*index=5...) while((s32[]{:T(128)}, f32[128,512]{1,0:T(8,128)S(1)}, ...), condition=%wide.region_7.8_spmd.clone, body=%wide.region_6.7_spmd.clone.sunk | while | flops 269746304 | bytes 3438348 | solution.py:153
  424.0 2.0 convolution_add_fusion.5
  426.1 1.9 convolution_add_fusion.4
  429.5 1.9 convolution_add_fusion.5
  431.5 1.9 convolution_add_fusion.4
  434.9 1.9 convolution_add_fusion.5
  436.9 1.9 convolution_add_fusion.4
  440.2 1.9 convolution_add_fusion.5
  442.3 1.9 convolution_add_fusion.4
  445.6 1.9 convolution_add_fusion.5
  447.6 1.9 convolution_add_fusion.4
  450.9 1.9 convolution_add_fusion.5
  453.0 1.9 convolution_add_fusion.4
  456.3 1.9 convolution_add_fusion.5
  458.4 1.9 convolution_add_fusion.4
  461.7 1.9 convolution_add_fusion.5
  463.7 1.9 convolution_add_fusion.4
  467.0 1.9 convolution_add_fusion.5
  469.1 1.9 convolution_add_fusion.4
  472.4 1.9 convolution_add_fusion.5
  474.5 1.9 convolution_add_fusion.4
  477.8 1.9 convolution_add_fusion.5
  483.2 1.9 convolution_add_fusion.5
  485.3 1.9 convolution_add_fusion.4
  488.6 1.9 convolution_add_fusion.5
  490.6 1.9 convolution_add_fusion.4
  493.9 1.9 convolution_add_fusion.5
  496.0 1.9 convolution_add_fusion.4
  499.3 1.9 convolution_add_fusion.5
  501.3 1.9 convolution_add_fusion.4
  504.7 1.9 convolution_add_fusion.5
  506.7 1.9 convolution_add_fusion.4
  509.2 14.4 %all_to_all.21 = f32[2,256,256]{2,1,0:T(8,128)S(1)} all-to-all(f32[2,256,256]{2,1,0:T(8,128)S(1)} %copy.28), channel_id=1, replica_groups=mesh['batch_0'=8,'batch_1'=4,'batch_2'=2,'batch_3'=2,'rep'=2] {'rep'}, dimensions={0} | all-to-all | bytes 1048576 | tf_op jit(solution)/shard_map/all_to_all | solution.py:131
  (285 shorter events, 69.6 us)
Async XLA Ops:
  19.8 14.9 %copy-start = (s32[16384]{0:T(1024)S(1)}, s32[16384]{0:T(1024)}, u32[]{:S(2)}) copy-start(s32[16384]{0:T(1024)} %param.9) | copy-start | bytes 196612
  19.8 249.3 %all-to-all-start = ((bf16[128,64,512]{2,1,0:T(8,128)(2,1)}), bf16[128,64,512]{2,1,0:T(8,128)(2,1)}, u32[]{:S(2)}, u32[]{:S(2)}) async-start(bf16[128,64,512]{2,1,0:T(8,128)(2,1)} %stack.2), calls=%async_computation | async-start | bytes 16777216 | tf_op jit(solution)/shard_map/all_to_all | solution.py:15
  33.8 377.4 %all-gather.15.cloned.1.call-start = ((), (), s32[]{:S(2)}) async-start(), calls=%async_computation.4 | async-start | bytes 16908288 | tf_op jit(solution)/shard_map/all_gather | solution.py:30
  323.2 48.9 %all-to-all-start.1 = ((f32[2,2,128]{2,1,0:T(2,128)}), f32[2,2,128]{2,1,0:T(2,128)S(1)}, u32[]{:S(2)}, u32[]{:S(2)}) async-start(f32[2,2,128]{2,1,0:T(2,128)} %broadcast_in_dim.21), calls=%async_computation.1 | async-start | bytes 4096 | tf_op jit(solution)/shard_map/all_to_all | solution.py:39
  372.8 37.6 %all-to-all-start.2 = ((f32[2,1,8192]{2,1,0:T(1,128)}), f32[2,1,8192]{2,1,0:T(1,128)S(1)}, u32[]{:S(2)}, u32[]{:S(2)}) async-start(f32[2,1,8192]{2,1,0:T(1,128)} %broadcast_in_dim.22), calls=%async_computation.2 | async-start | bytes 131072 | tf_op jit(solution)/shard_map/all_to_all | solution.py:39
Sparse Core Ops, SparseCore 0:
  37.1 325.7 all-gather.14
